TPU v7x, 32 devices: a whole 2x2x4 slice. The times are simulated.
32 devices in a mesh: leaf: 4 (over y, x), blk: 8 (over z, core).
Axes of the slice: x: 2, y: 2, z: 4, core: 2. Of those that a mesh axis runs over, the one named last changes fastest.
Arguments:
- leaf_rhs: bfloat16 [10240, 256], P(('leaf', 'blk')), may hold values from -6 to 6
- leaf_inverse: bfloat16 [10240, 2560], P(('leaf', 'blk')), may hold values from -0.125 to 0.125
- leaf_lower: bfloat16 [4096, 2560], P(('leaf', 'blk')), may hold values from -0.125 to 0.125
- sep_rhs: bfloat16 [2, 2048, 256], P(None, ('leaf', 'blk')), may hold values from -6 to 6
- sep_inverse: bfloat16 [2048, 3072], P(('leaf', 'blk'))
- sep_lower: bfloat16 [4096, 1024], P(('leaf', 'blk'))
- slot_map: int32 [2, 32, 2], P(None, ('leaf', 'blk')), may hold values from 0 to 5, as said below
Outputs:
- leaf_solution: bfloat16 [10240, 256], P(('leaf', 'blk'))
- sep_solution: bfloat16 [2, 2048, 256], P(None, ('leaf', 'blk'))
Inputs may be any that keep to these rules, and one draw needn't show every extreme that they name: For every level below the top, slot_map[h-1, q] holds two different numbers of 0 to 5; at the top level it holds 0 and 1 in some order.
All inputs are finite; a program needn't handle non-finite values.
Results may differ from a plain program's by a relative error of at most 0.015.
Values may be sent and summed in bfloat16 or wider, within the bound.
A program may use at most 128 MiB of HBM per device.

v0:
```python
import functools

import jax
import jax.numpy as jnp
from jax import lax
from jax.experimental import pallas as pl
from jax.experimental.pallas import tpu as pltpu
from jax.sharding import PartitionSpec as P

CHUNKS = 2
MESH = pl.DeviceIdType.MESH
F32 = jnp.float32
BF16 = jnp.bfloat16


def flipped(value, mask):
    bit = 0
    while 2**bit <= mask:
        if mask >> bit & 1:
            value = value + (1 - 2 * (value // 2**bit % 2)) * 2**bit
        bit += 1
    return value


class Links:
    def __init__(self, send_sems, recv_sems):
        self.send_sems, self.recv_sems = send_sems, recv_sems
        self.count = 0
        self.started = []

    def site(self):
        self.count += 1
        return self.count - 1

    def copy(self, site, source, target, device):
        return pltpu.make_async_remote_copy(
            src_ref=source,
            dst_ref=target,
            send_sem=self.send_sems.at[site],
            recv_sem=self.recv_sems.at[site],
            device_id=device,
            device_id_type=MESH,
        )

    def send(self, site, block, device, source=None):
        copy = self.copy(site, block if source is None else source, block, device)
        copy.start()

    def later(self, site, block, device, valid=None):
        self.started.append((site, block, device, valid))

    def arrived(self, site, block, device):
        self.copy(site, block, block, device).wait_recv()

    def drain(self):
        for site, block, device, valid in self.started:
            if valid is None:
                self.copy(site, block, block, device).wait_send()
            else:
                @pl.when(valid)
                def _(site=site, block=block, device=device):
                    self.copy(site, block, block, device).wait_send()


def products_of(levels, pivots):
    found = []
    for height in range(1, levels + 1):
        found.append((height, pivots))
        if height < levels:
            found.append((height, 2 * pivots))
    return found


def plan_sites(leaves, blks, levels, chunks):
    chips = blks // 2
    per_chunk = 2 * (4 * chips - 3)
    shared = 0
    for height, _ in products_of(levels, 1):
        others = 2 * 2**height - 1
        per_chunk += chips - 1 + others + 1
        shared += others
    return per_chunk * chunks + shared


def kernel(dims, *refs):
    leaves, blks, levels, chunks = dims
    (rhs_hbm, inv_hbm, low_hbm, srhs_hbm, sinv_hbm, slow_hbm, slots_hbm) = refs[:7]
    leaf_out, sep_out = refs[7:9]
    (inv, low, srhs, xbuf, ybuf, acc, upd, slots, send_sems, recv_sems, local_sems) = refs[9:20]
    rest = refs[20:]
    sent, got = rest[: 2 * levels : 2], rest[1 : 2 * levels : 2]
    groups = [rest[at : at + 4] for at in range(2 * levels, len(rest), 4)]

    leaf = lax.axis_index("leaf")
    blk = lax.axis_index("blk")
    chips = blks // 2
    chip = blk // 2
    core = blk % 2
    other = blk + 1 - 2 * core
    rows = rhs_hbm.shape[0]
    columns = rhs_hbm.shape[1]
    width = columns // chunks
    pivots = srhs_hbm.shape[1]
    links = Links(send_sems, recv_sems)

    def blk_of(some_chip):
        return some_chip * 2 + core

    loads = []
    for index in range(chunks):
        loads.append(
            pltpu.make_async_copy(
                rhs_hbm.at[:, pl.ds(index * width, width)],
                xbuf.at[index, pl.ds(pl.multiple_of(blk * rows, 16), rows)],
                local_sems.at[index],
            )
        )
    weight_loads = [
        pltpu.make_async_copy(source, target, local_sems.at[chunks + index])
        for index, (source, target) in enumerate(
            ((inv_hbm, inv), (low_hbm, low), (srhs_hbm, srhs), (slots_hbm, slots))
        )
    ]
    for load in loads + weight_loads:
        load.start()
    for vectors, _, _, _ in groups:
        vectors[...] = jnp.zeros_like(vectors)

    barrier = pltpu.get_barrier_semaphore()
    near = [(leaf, other)]
    near += [
        (flipped(leaf, mask), side) for mask in range(1, 2**levels) for side in (blk, other)
    ]
    ends = [(chip > 0, (leaf, blk - 2)), (chip < chips - 1, (leaf, blk + 2))]
    for valid, peer in ends:
        @pl.when(valid)
        def _(peer=peer):
            pl.semaphore_signal(barrier, inc=1, device_id=peer, device_id_type=MESH)
    for peer in near:
        pl.semaphore_signal(barrier, inc=1, device_id=peer, device_id_type=MESH)
    has_both = (chip + chips - 1) // chips + (2 * chips - 2 - chip) // chips
    pl.semaphore_wait(barrier, len(near) + has_both)

    def line_product(buf, weights, total, ready):
        depth = 2 * rows

        def piece(some_chip, some_core):
            return buf.at[pl.ds(pl.multiple_of((some_chip * 2 + some_core) * rows, 16), rows)]

        def chip_dot(some_chip):
            start = pl.multiple_of(some_chip * depth, 128)
            return jnp.dot(
                weights[:, pl.ds(start, depth)],
                buf[pl.ds(start, depth)],
                preferred_element_type=F32,
            )

        go_left = [links.site() for _ in range(chips - 1)]
        go_right = [links.site() for _ in range(chips - 1)]
        across = [links.site() for _ in range(2 * chips - 1)]
        left, right = (leaf, blk - 2), (leaf, blk + 2)
        mine = piece(chip, core)
        across_device = (leaf, other)

        has_left, has_right = chip > 0, chip < chips - 1

        @pl.when(has_left)
        def _():
            links.send(go_left[0], mine, left)

        @pl.when(has_right)
        def _():
            links.send(go_right[0], mine, right)

        links.send(across[0], mine, across_device)
        links.later(go_left[0], mine, left, has_left)
        links.later(go_right[0], mine, right, has_right)
        links.later(across[0], mine, across_device)
        yield
        links.arrived(across[0], piece(chip, 1 - core), across_device)
        ready()
        total[...] = chip_dot(chip)
        for step in range(chips - 1):
            yield
            from_right, from_left = chip + step + 1, chip - step - 1
            right_valid, left_valid = from_right < chips, from_left >= 0

            @pl.when(right_valid)
            def _():
                links.arrived(go_left[step], piece(from_right, core), right)
                if step + 1 < chips - 1:
                    @pl.when(has_left)
                    def _():
                        links.send(go_left[step + 1], piece(from_right, core), left)
                links.send(across[1 + step], piece(from_right, core), across_device)

            @pl.when(left_valid)
            def _():
                links.arrived(go_right[step], piece(from_left, core), left)
                if step + 1 < chips - 1:
                    @pl.when(has_right)
                    def _():
                        links.send(go_right[step + 1], piece(from_left, core), right)
                links.send(across[chips + step], piece(from_left, core), across_device)

            if step + 1 < chips - 1:
                links.later(
                    go_left[step + 1], mine, left, jnp.logical_and(right_valid, has_left)
                )
                links.later(
                    go_right[step + 1], mine, right, jnp.logical_and(left_valid, has_right)
                )
            links.later(across[1 + step], mine, across_device, right_valid)
            links.later(across[chips + step], mine, across_device, left_valid)
            yield

            @pl.when(right_valid)
            def _():
                links.arrived(across[1 + step], piece(from_right, 1 - core), across_device)

            @pl.when(left_valid)
            def _():
                links.arrived(across[chips + step], piece(from_left, 1 - core), across_device)

            first = jnp.where(right_valid, 0, 1)
            last = jnp.where(left_valid, 2, 1)

            def add(side, carry):
                total[...] += chip_dot(chip + (1 - 2 * side) * (step + 1))
                return carry

            lax.fori_loop(first, last, add, 0)

    wanted = products_of(levels, pivots)
    section = pivots * blks
    fetched, own_blocks = [], []

    def exchange_weights():
        for at, (height, height_rows) in enumerate(wanted):
            source = sinv_hbm if height_rows == pivots else slow_hbm
            span = 2**height
            weights = groups[at][1]
            offset = section * (span - 2)
            sites = {}
            for mask in range(span):
                local = flipped(leaf, mask) % span
                start = pl.multiple_of(offset + local * section, 128)
                block = source.at[:, pl.ds(start, section)]
                for side in range(2):
                    spot = weights.at[pl.ds((2 * mask + side) * height_rows, height_rows)]
                    if mask == 0 and side == 0:
                        own = pltpu.make_async_copy(
                            block, spot, local_sems.at[chunks + 4 + at]
                        )
                        own.start()
                        own_blocks.append(own)
                        continue
                    device = (flipped(leaf, mask), other if side else blk)
                    site = links.site()
                    links.send(site, spot, device, source=block)
                    links.later(site, spot, device)
                    sites[site] = (spot, device)
            fetched.append(sites)

    def weights_ready(at):
        if at in waited:
            return
        waited.add(at)
        own_blocks[at].wait()
        for site, (spot, device) in fetched[at].items():
            links.arrived(site, spot, device)

    def group_product(at, index, value):
        height, height_rows = wanted[at]
        span = 2**height
        vectors, weights, going, coming = groups[at]
        vectors = vectors.at[index]

        def piece(some_chip):
            return vectors.at[
                pl.ds(pl.multiple_of((some_chip * 2 + core) * pivots, 16), pivots)
            ]

        mine = pl.ds(pl.multiple_of(blk * pivots, 16), pivots)
        vectors[mine] = value
        along = [links.site() for _ in range(1, chips)]
        for step in range(chips - 1, 0, -1):
            device = (leaf, blk_of((chip + step) % chips))
            links.send(along[step - 1], piece(chip), device)
            links.later(along[step - 1], piece(chip), device)
        yield
        weights_ready(at)
        for step in range(1, chips):
            source = (chip + chips - step) % chips
            links.arrived(along[step - 1], piece(source), (leaf, blk_of(source)))
        parts = jnp.dot(weights[...], vectors[...], preferred_element_type=F32)
        going[index] = parts.astype(BF16)
        pending = []
        for spot in range(2 * span - 1, 0, -1):
            mask, side = spot // 2, spot % 2
            device = (flipped(leaf, mask), other if side else blk)
            block = pl.ds(spot * height_rows, height_rows)
            site = links.site()
            target = coming.at[index, block]
            links.send(site, target, device, source=going.at[index, block])
            links.later(site, target, device)
            pending.append((site, block, target, device))
        total = parts[:height_rows]
        yield
        for site, block, target, device in reversed(pending):
            links.arrived(site, target, device)
            total = total + coming[index, block].astype(F32)
        products[index] = total

    products = {}
    waited = set()

    def once(index):
        def wait():
            if (index,) not in waited:
                waited.add((index,))
                weight_loads[index].wait()

        return wait

    def chain(index):
        cols = pl.ds(index * width, width)
        own = pl.ds(pl.multiple_of(blk * rows, 16), rows)
        loads[index].wait()
        yield from line_product(xbuf.at[index], inv, acc.at[index], once(0))
        value = acc[index].astype(BF16)
        ybuf[index, own] = value
        leaf_out[:, cols] = value
        yield from line_product(ybuf.at[index], low, upd.at[index], once(1))
        upd[index] = -upd[index]
        for wait in (once(2), once(3)):
            wait()
        at = 0
        for height in range(1, levels + 1):
            at_root = height == levels
            kept = 1 if at_root else 3

            def mixed(slot):
                total = None
                for part in range(2):
                    weight = jnp.where(slots[height - 1, 0, part] == slot, 1.0, 0.0).astype(F32)
                    term = weight * upd[index, pl.ds(part * pivots, pivots)]
                    total = term if total is None else total + term
                return total

            partner = (flipped(leaf, 2 ** (height - 1)), blk)
            outgoing, incoming = sent[height - 1].at[index], got[height - 1].at[index]
            for first, last in ((0, 1), (1, kept)):
                if first == last:
                    continue
                for slot in range(first, last):
                    outgoing[pl.ds(slot * pivots, pivots)] = mixed(kept + slot).astype(BF16)
                part = pl.ds(first * pivots, (last - first) * pivots)
                site = links.site()
                links.send(site, incoming.at[part], partner, source=outgoing.at[part])
                links.later(site, incoming.at[part], partner)
                if first == 0:
                    first_site = site
                else:
                    rest_site, rest_part = site, part
            base = srhs[height - 1, :, cols].astype(F32) + mixed(0)
            yield
            head = pl.ds(0, pivots)
            links.arrived(first_site, incoming.at[head], partner)
            pivot = (base + incoming[head].astype(F32)).astype(BF16)
            yield from group_product(at, index, pivot)
            at += 1
            solved = products[index].astype(BF16)
            sep_out[height - 1, :, cols] = solved
            if not at_root:
                yield from group_product(at, index, solved)
                at += 1
                product = products[index]
                links.arrived(rest_site, incoming.at[rest_part], partner)
                keep = [mixed(slot) for slot in (1, 2)]
                for part in range(2):
                    upd[index, pl.ds(part * pivots, pivots)] = (
                        keep[part]
                        + incoming[pl.ds((1 + part) * pivots, pivots)].astype(F32)
                        - product[part * pivots : (part + 1) * pivots]
                    )

    running = [chain(index) for index in range(chunks)]
    started = False
    while running:
        alive = []
        for steps in running:
            try:
                next(steps)
                alive.append(steps)
            except StopIteration:
                pass
        running = alive
        if not started:
            started = True
            exchange_weights()
    assert links.count <= send_sems.shape[0]
    links.drain()


def hand_over(first, second, first_out, second_out, sems):
    copies = [
        pltpu.make_async_copy(first, first_out, sems.at[0]),
        pltpu.make_async_copy(second, second_out, sems.at[1]),
    ]
    for copy in copies:
        copy.start()
    for copy in copies:
        copy.wait()


def deliver(first, second):
    return pl.pallas_call(
        hand_over,
        out_shape=tuple(jax.ShapeDtypeStruct(x.shape, x.dtype) for x in (first, second)),
        in_specs=[pl.BlockSpec(memory_space=pltpu.VMEM)] * 2,
        out_specs=(pl.BlockSpec(memory_space=pltpu.HBM),) * 2,
        scratch_shapes=[pltpu.SemaphoreType.DMA((2,))],
        name="deliver",
    )(first, second)


def on_device(dims, leaf_rhs, leaf_inverse, leaf_lower, sep_rhs, sep_inverse, sep_lower, slot_map):
    leaves, blks, levels, chunks = dims
    rows, columns = leaf_rhs.shape
    width = columns // chunks
    pivots = sep_rhs.shape[1]
    updates = leaf_lower.shape[0]
    slot_shape = slot_map.shape
    sites = plan_sites(leaves, blks, levels, chunks)
    wanted = products_of(levels, pivots)
    scratch = [
        pltpu.VMEM(leaf_inverse.shape, BF16),
        pltpu.VMEM(leaf_lower.shape, BF16),
        pltpu.VMEM(sep_rhs.shape, BF16),
        pltpu.VMEM((chunks, rows * blks, width), BF16),
        pltpu.VMEM((chunks, rows * blks, width), BF16),
        pltpu.VMEM((chunks, rows, width), F32),
        pltpu.VMEM((chunks, updates, width), F32),
        pltpu.SMEM(slot_shape, jnp.int32),
        pltpu.SemaphoreType.DMA((sites,)),
        pltpu.SemaphoreType.DMA((sites,)),
        pltpu.SemaphoreType.DMA((chunks + 4 + len(wanted),)),
    ]
    for height in range(1, levels + 1):
        kept = 1 if height == levels else 3
        scratch += [pltpu.VMEM((chunks, kept * pivots, width), BF16)] * 2
    section = pivots * blks
    for height, height_rows in wanted:
        members = 2 * 2**height * height_rows
        scratch += [
            pltpu.VMEM((chunks, section, width), BF16),
            pltpu.VMEM((members, section), BF16),
            pltpu.VMEM((chunks, members, width), BF16),
            pltpu.VMEM((chunks, members, width), BF16),
        ]
    results = pl.pallas_call(
        functools.partial(kernel, dims),
        out_shape=(
            jax.ShapeDtypeStruct((rows, columns), BF16),
            jax.ShapeDtypeStruct(sep_rhs.shape, BF16),
        ),
        in_specs=[pl.BlockSpec(memory_space=pltpu.HBM)] * 7,
        out_specs=(pl.BlockSpec(memory_space=pltpu.VMEM),) * 2,
        scratch_shapes=scratch,
        compiler_params=pltpu.CompilerParams(
            collective_id=0, has_side_effects=True, vmem_limit_bytes=60 * 2**20
        ),
        name="substitution",
    )(leaf_rhs, leaf_inverse, leaf_lower, sep_rhs, sep_inverse, sep_lower, slot_map)
    return deliver(*results)


def solution(mesh):
    leaves, blks = mesh.shape["leaf"], mesh.shape["blk"]

    def body(*args):
        dims = (leaves, blks, args[3].shape[0], CHUNKS)
        return on_device(dims, *args)

    return jax.shard_map(
        body,
        mesh=mesh,
        in_specs=(
            P(("leaf", "blk"), None),
            P(("leaf", "blk"), None),
            P(("leaf", "blk"), None),
            P(None, ("leaf", "blk"), None),
            P(("leaf", "blk"), None),
            P(("leaf", "blk"), None),
            P(None, ("leaf", "blk"), None),
        ),
        out_specs=(P(("leaf", "blk"), None), P(None, ("leaf", "blk"), None)),
        check_vma=False,
    )
```

profile of v0, /device:TPU:0, one launch (start us, length us, event | category | flops | bytes accessed | tf_op | source)
XLA Modules:
  0.0 67.5 jit_solution(424368405010543194)
XLA Ops:
  0.6 65.2 %substitution.1 = (bf16[320,256]{1,0:T(8,128)(2,1)}, bf16[2,64,256]{2,1,0:T(8,128)(2,1)}) custom-call(bf16[320,256]{1,0:T(8,128)(2,1)} %refs_0_.1, bf16[320,2560]{1,0:T(8,128)(2,1)} %refs_1_.1, bf16[128,2560]{1,0:T(8,128)(2,1)} %refs_2_.1, bf16[2,64,256]{2,1,0:T(8,128)(2,1)} %refs_3_.1, bf16[64,3072]{1,0:T(8,128)(2,1)} %refs_4_.1, ...), custom_call_target="tpu_custom_call" | custom-call | tf_op jit(solution)/shard_map/substitution/pallas_call | solution.py:462
  65.9 1.6 %deliver.1 = (bf16[320,256]{1,0:T(8,128)(2,1)}, bf16[2,64,256]{2,1,0:T(8,128)(2,1)}) custom-call(bf16[320,256]{1,0:T(8,128)(2,1)} %get-tuple-element.4.first, bf16[2,64,256]{2,1,0:T(8,128)(2,1)} %get-tuple-element.5.second), custom_call_target="tpu_custom_call" | custom-call | tf_op jit(solution)/shard_map/deliver/pallas_call | solution.py:418
where the time goes:
time: 67.6 us; the launch traced here: 67.5 us
  Pallas kernels  66.8 us (99%)
    pallas_call x1, Pallas kernels, on_device(): pl.pallas_call(functools.partial(kernel, dims), out_shape=(jax.ShapeDtype...  65.2 us
    pallas_call x1, Pallas kernels, deliver(): pl.pallas_call(hand_over, out_shape=tuple((jax.ShapeDtypeStruct(x.shape,...  1.62 us

commit v1 on v0

--- a/solution.py
+++ b/solution.py
@@ -422,7 +422,7 @@
         out_specs=(pl.BlockSpec(memory_space=pltpu.HBM),) * 2,
         scratch_shapes=[pltpu.SemaphoreType.DMA((2,))],
         name="deliver",
-    )(first, second)
+    )(*[pltpu.with_memory_space_constraint(x, pltpu.VMEM) for x in (first, second)])
 
 
 def on_device(dims, leaf_rhs, leaf_inverse, leaf_lower, sep_rhs, sep_inverse, sep_lower, slot_map):
@@ -462,8 +462,8 @@
     results = pl.pallas_call(
         functools.partial(kernel, dims),
         out_shape=(
-            jax.ShapeDtypeStruct((rows, columns), BF16),
-            jax.ShapeDtypeStruct(sep_rhs.shape, BF16),
+            pltpu.VMEM((rows, columns), BF16),
+            pltpu.VMEM(sep_rhs.shape, BF16),
         ),
         in_specs=[pl.BlockSpec(memory_space=pltpu.HBM)] * 7,
         out_specs=(pl.BlockSpec(memory_space=pltpu.VMEM),) * 2,

time: 67.6 us -> 66 us (0.976)
  Pallas kernels: 66.8 us -> 65.3 us
    pallas_call x1, Pallas kernels: 1.62 us -> 0.7 us  [deliver(): pl.pallas_call(hand_over, out_shape=tuple((jax.ShapeDtypeStruct(x.shape,...]
where the time goes in v1:
time: 66 us; the launch traced here: 65.9 us
  Pallas kernels  65.3 us (99%)
    pallas_call x1, Pallas kernels, on_device(): pl.pallas_call(functools.partial(kernel, dims), out_shape=(pltpu.VMEM((ro...  64.5 us

profile of v1, /device:TPU:0, one launch (start us, length us, event | category | flops | bytes accessed | tf_op | source)
XLA Modules:
  0.0 65.9 jit_solution(3900947773691870725)
XLA Ops:
  0.6 64.5 %substitution.1 = (bf16[320,256]{1,0:T(8,128)(2,1)S(1)}, bf16[2,64,256]{2,1,0:T(8,128)(2,1)S(1)}) custom-call(bf16[320,256]{1,0:T(8,128)(2,1)} %refs_0_.1, bf16[320,2560]{1,0:T(8,128)(2,1)} %refs_1_.1, bf16[128,2560]{1,0:T(8,128)(2,1)} %refs_2_.1, bf16[2,64,256]{2,1,0:T(8,128)(2,1)} %refs_3_.1, bf16[64,3072]{1,0:T(8,128)(2,1)} %refs_4_.1, ...), custom_call_target="tpu_custom_call" | custom-call | tf_op jit(solution)/shard_map/substitution/pallas_call | solution.py:462
  65.2 0.7 %deliver.1 = (bf16[320,256]{1,0:T(8,128)(2,1)}, bf16[2,64,256]{2,1,0:T(8,128)(2,1)}) custom-call(bf16[320,256]{1,0:T(8,128)(2,1)S(1)} %get-tuple-element.4.first, bf16[2,64,256]{2,1,0:T(8,128)(2,1)S(1)} %get-tuple-element.5.second), custom_call_target="tpu_custom_call" | custom-call | tf_op jit(solution)/shard_map/deliver/pallas_call | solution.py:418
